TPU v7x, 32 devices: a whole 2x2x4 slice. The times are simulated.
32 devices in a mesh: seq: 4 (over y, core), blk: 8 (over z, x).
Axes of the slice: x: 2, y: 2, z: 4, core: 2. Of those that a mesh axis runs over, the one named last changes fastest.
Arguments:
- kv_cache: bfloat16 [4, 2, 16, 4096, 1024], P(None, None, None, ('seq', 'blk')), may hold values from -18 to 18, as said below
- queries: bfloat16 [4, 128, 1024], P(None, 'blk'), may hold values from -400 to 400
- fresh_key_value: bfloat16 [4, 2, 128, 128], P(None, None, 'blk'), may hold values from -70 to 70
- lengths: int32 [16], replicated, may hold values from 1 to 4096, 49152 in all
Outputs:
- quant_cache: bfloat16 [4, 2, 128, 4096, 128], P(None, None, 'blk', 'seq')
- block_scale: float32 [4, 2, 128, 32], P(None, None, 'blk', 'seq')
- attended: bfloat16 [4, 128, 1024], P(None, 'blk')
Inputs may be any that keep to these rules, and one draw needn't show every extreme that they name: `kv_cache`: each entry is a random value times a factor drawn for its position and head. `lengths`: every sequence has at least one live position, and some sequence uses all 4096.
All inputs are finite; a program needn't handle non-finite values.
Results may differ from a plain program's by a relative error of at most 0.003.
The roundings to bfloat16 on the way count: a program that leaves them out, or rounds other values in their place, can miss the bound.
Values may be sent and summed in bfloat16 or wider, within the bound.
No kernel may reach another device: no remote copies, remote signals or barrier semaphores. Data moves between devices by JAX's collectives and lax.ppermute only.
A program may use at most 192 MiB of HBM per device.

v0:
```python
import jax
import jax.numpy as jnp
from jax import lax
from jax.sharding import PartitionSpec as P

HEAD_DIM = 128
QUERY_GROUP = 8
BLOCK = 128


def on_device(kv_cache, queries, fresh_key_value, lengths):
    layers, _, batch, local_rows, width = kv_cache.shape
    heads = width // HEAD_DIM
    blk_count = lax.axis_size("blk")
    blk_place = lax.axis_index("blk")
    pairs_here = heads * batch // blk_count
    seq_rows = local_rows * blk_count
    blocks_here = seq_rows // BLOCK
    arranged = kv_cache.reshape(layers, 2, batch, local_rows, heads, HEAD_DIM).transpose(
        0, 1, 4, 2, 3, 5
    )
    arranged = arranged.reshape(layers, 2, heads * batch, local_rows, HEAD_DIM)
    pair_start = blk_place * pairs_here
    moved = lax.all_to_all(arranged, "blk", split_axis=2, concat_axis=3, tiled=True)
    grouped = moved.reshape(layers, 2, pairs_here, blocks_here, BLOCK, HEAD_DIM)
    block_scale = (
        jnp.maximum(jnp.max(jnp.abs(grouped), axis=(4, 5)).astype(jnp.float32), 1.0) / 127.0
    )
    quant = (grouped.astype(jnp.float32) / block_scale[..., None, None]).astype(jnp.bfloat16)
    quant = quant.reshape(layers, 2, pairs_here, seq_rows, HEAD_DIM)
    seq_start = lax.axis_index("seq") * seq_rows
    pair_len = lax.dynamic_slice_in_dim(jnp.tile(lengths, heads), pair_start, pairs_here)
    positions = seq_start + jnp.arange(seq_rows, dtype=jnp.int32).reshape(blocks_here, BLOCK)
    valid = positions[None] < pair_len[:, None, None]
    inverse = 1.0 / jnp.sqrt(jnp.float32(HEAD_DIM))
    grouped_queries = queries.reshape(layers, pairs_here, QUERY_GROUP, HEAD_DIM)
    peaks = []
    totals = []
    sums = []
    for layer in range(layers):
        raw = jnp.einsum(
            "pgd,prd->pgr",
            grouped_queries[layer],
            quant[layer, 0],
            preferred_element_type=jnp.float32,
        )
        scores = (
            raw.reshape(pairs_here, QUERY_GROUP, blocks_here, BLOCK)
            * block_scale[layer, 0][:, None, :, None]
            * inverse
        )
        masked = jnp.where(valid[:, None], scores, -1e30)
        block_top = jnp.max(masked, axis=-1)
        weight = jnp.where(valid[:, None], jnp.exp(masked - block_top[..., None]), 0.0)
        block_total = jnp.sum(weight, axis=-1)
        rounded = (weight * block_scale[layer, 1][:, None, :, None]).astype(jnp.bfloat16)
        values = quant[layer, 1].reshape(pairs_here, blocks_here, BLOCK, HEAD_DIM)
        block_sum = jnp.einsum(
            "pgnt,pntd->pgnd", rounded, values, preferred_element_type=jnp.float32
        )
        local_top = jnp.max(block_top, axis=-1)
        scale_factor = jnp.exp(block_top - local_top[..., None])
        peaks.append(local_top)
        totals.append(jnp.sum(scale_factor * block_total, axis=-1))
        sums.append(jnp.sum(scale_factor[..., None] * block_sum, axis=2))
    peak = jnp.stack(peaks)
    total = jnp.stack(totals)
    weighted = jnp.stack(sums)
    shared_top = lax.pmax(peak, "seq")
    scale_factor = jnp.exp(peak - shared_top)
    total, weighted = lax.psum((total * scale_factor, weighted * scale_factor[..., None]), "seq")
    peak = shared_top
    own = (
        jnp.einsum(
            "lpgd,lpd->lpg",
            grouped_queries,
            fresh_key_value[:, 0],
            preferred_element_type=jnp.float32,
        )
        * inverse
    )
    top = jnp.maximum(peak, own)
    cache_w = jnp.exp(peak - top)
    own_w = jnp.exp(own - top)
    numer = (
        weighted * cache_w[..., None]
        + own_w[..., None] * fresh_key_value[:, 1].astype(jnp.float32)[:, :, None, :]
    )
    denom = total * cache_w + own_w
    attended = (
        (numer / denom[..., None])
        .reshape(layers, pairs_here, QUERY_GROUP * HEAD_DIM)
        .astype(jnp.bfloat16)
    )
    return (quant, block_scale, attended)


def solution(mesh):
    in_specs = (
        P(None, None, None, ("seq", "blk"), None),
        P(None, "blk", None),
        P(None, None, "blk", None),
        P(),
    )
    out_specs = (
        P(None, None, "blk", "seq", None),
        P(None, None, "blk", "seq"),
        P(None, "blk", None),
    )
    return jax.shard_map(
        on_device, mesh=mesh, in_specs=in_specs, out_specs=out_specs, check_vma=False
    )
```

profile of v0, /device:TPU:0, one launch (start us, length us, event | category | flops | bytes accessed | tf_op | source)
XLA Modules:
  0.0 1028.5 jit_solution(197977357570739834)
XLA Ops:
  7.2 43.9 %copy.101 = bf16[4,2,16,128,1024]{3,4,2,1,0:T(8,128)(2,1)} copy(bf16[4,2,16,128,1024]{4,3,2,1,0:T(8,128)(2,1)} %param.4) | data formatting | bytes 67108864 | tf_op args[0]
  51.0 42.3 %copy.102 = bf16[4,2,8,16,128,128]{5,4,3,2,1,0:T(8,128)(2,1)} copy(bf16[4,2,8,16,128,128]{4,5,2,3,1,0:T(8,128)(2,1)} %bitcast.243) | data formatting | bytes 67108864 | tf_op jit(solution)/shard_map/transpose | solution.py:19
  93.4 22.9 %copy.103 = bf16[4,2,128,128,128]{4,3,1,0,2:T(8,128)(2,1)} copy(bf16[4,2,128,128,128]{4,3,2,1,0:T(8,128)(2,1)} %bitcast.241) | data formatting | bytes 67108864 | tf_op jit(solution)/shard_map/reshape | solution.py:22
  116.3 7.4 all-to-all-start
  123.7 0.0 all-reduce.2.cloned.1.call-start
  123.8 0.1 tile.10
  124.0 0.2 fusion.70
  124.2 0.1 copy.132
  124.3 0.1 dynamic_slice.3
  124.4 0.1 broadcast_compare_fusion.1
  124.5 0.1 broadcast_compare_fusion
  124.6 723.3 %all-to-all-done = bf16[4,2,128,128,128]{4,3,1,0,2:T(8,128)(2,1)} async-done(((bf16[4,2,128,128,128]{4,3,1,0,2:T(8,128)(2,1)}), bf16[4,2,128,128,128]{4,3,1,0,2:T(8,128)(2,1)}, u32[]{:S(2)}, u32[]{:S(2)}) %all-to-all-start) | async-done | bytes 33554464 | tf_op jit(solution)/shard_map/all_to_all | solution.py:24
  847.9 11.5 %abs_reduce_fusion = bf16[4,2,128]{1,0,2:T(4,128)(2,1)S(1)} fusion(bf16[4,2,128,128,128]{4,3,1,0,2:T(8,128)(2,1)} %all-to-all-done), kind=kLoop, calls=%fused_computation.3 | loop fusion | flops 33553408 | bytes 33556480 | tf_op jit(solution)/shard_map/reduce_max | solution.py:27
  859.3 0.1 maximum_multiply_fusion.1
  859.4 0.3 copy.105
  859.7 0.1 copy.107
  859.8 23.0 %copy.104 = bf16[4,2,128,128,128]{4,3,2,1,0:T(8,128)(2,1)} copy(bf16[4,2,128,128,128]{4,3,1,0,2:T(8,128)(2,1)} %all-to-all-done) | data formatting | bytes 67108864 | tf_op jit(solution)/shard_map/all_to_all | solution.py:24
  882.8 23.3 %fusion.1 = bf16[4,2,16,8,128,128]{5,4,2,3,1,0:T(8,128)(2,1)} fusion(bf16[4,2,8,16,128,128]{5,4,3,2,1,0:T(8,128)(2,1)} %bitcast.242, f32[4,2,16,8]{2,3,1,0:T(8,128)S(1)} %bitcast.258), kind=kLoop, calls=%fused_computation.2 | loop fusion | flops 50331648 | bytes 67112960 | tf_op jit(solution)/shard_map/convert_element_type | solution.py:29
  906.1 22.9 %copy.106 = bf16[4,2,16,8,128,128]{5,4,3,2,1,0:T(8,128)(2,1)} copy(bf16[4,2,16,8,128,128]{5,4,2,3,1,0:T(8,128)(2,1)} %fusion.1) | data formatting | bytes 67108864 | tf_op jit(solution)/shard_map/convert_element_type | solution.py:29
  929.0 12.2 %fusion.90 = (bf16[1,1,16,1024,128]{4,3,2,1,0:T(8,128)(2,1)}, bf16[1,1,16,1024,128]{4,3,2,1,0:T(8,128)(2,1)}, bf16[1,1,16,1024,128]{4,3,2,1,0:T(8,128)(2,1)}, bf16[1,1,16,1024,128]{4,3,2,1,0:T(8,128)(2,1)}) fusion(bf16[4,2,16,1024,128]{4,3,2,1,0:T(8,128)(2,1)} %bitcast.244), kind=kLoop, calls=%fused_computation.153 | loop fusion | bytes 33554432 | tf_op jit(solution)/shard_map/slice | solution.py:57
  941.2 3.4 fusion.2
  944.5 3.4 fusion.3
  947.9 0.1 copy.110
  948.0 0.1 copy.113
  948.0 0.1 copy.116
  948.1 0.1 mul.279
  948.2 0.1 mul.265
  948.3 0.1 mul.251
  948.4 0.1 mul.237
  948.5 3.5 fusion.38
  952.0 3.1 fusion.34
  955.1 0.6 fusion.33
  955.7 0.1 copy.119
  955.8 0.1 copy.120
  955.9 0.1 copy.121
  955.9 0.1 copy.122
  956.0 10.1 pmax.7
  966.1 1.5 fusion.35
  967.6 0.1 multiply_reduce_fusion.2
  967.7 0.1 copy.126
  967.7 0.1 copy.127
  967.8 0.1 multiply_reduce_fusion
  967.9 0.1 copy.128
  967.9 0.1 copy.129
  968.0 10.3 %psum.15 = f32[4,16,8]{1,2,0:T(8,128)S(1)} all-reduce(f32[4,16,8]{1,2,0:T(8,128)S(1)} %get-tuple-element.17), channel_id=1, replica_groups=mesh['seq'=4,'blk'=8] {'seq'}, use_global_device_ids=true, to_apply=%region_23.24 | all-reduce | flops 512 | bytes 4096 | tf_op jit(solution)/shard_map/psum | solution.py:71
  978.3 0.1 copy.123
  978.4 0.1 copy.109
  978.5 0.1 copy.112
  978.5 0.1 copy.115
  978.6 0.1 copy.118
  978.7 3.6 fusion.13
  982.3 1.3 fusion.12
  983.6 0.9 copy-done.1
  984.5 1.3 fusion.11
  985.8 0.2 copy-done
  986.0 1.3 fusion.10
  987.3 0.8 maximum_multiply_fusion
  988.2 0.0 all-reduce.2.cloned.1.call-update
  988.2 0.1 copy.124
  988.3 0.1 copy.125
  988.4 0.1 copy.130
  988.5 31.2 %all-reduce.2.cloned.1.call-done = f32[4,16,8,128]{3,2,1,0:T(8,128)} async-done(((f32[4,16,8,128]{3,2,1,0:T(8,128)}), f32[4,16,8,128]{3,2,1,0:T(8,128)}) %all-reduce.2.cloned.1.call-update) | async-done | bytes 262160 | tf_op jit(solution)/shard_map/psum | solution.py:71
  1019.7 1.2 divide_convert_fusion
  1020.9 0.7 convert_element_type.61
  (30 shorter events, 0.3 us)
Async XLA Ops:
  116.3 7.5 copy-start.6
  116.3 7.6 copy-start.3
  116.3 7.7 copy-start.5
  116.3 731.5 %all-to-all-start = ((bf16[4,2,128,128,128]{4,3,1,0,2:T(8,128)(2,1)}), bf16[4,2,128,128,128]{4,3,1,0,2:T(8,128)(2,1)}, u32[]{:S(2)}, u32[]{:S(2)}) async-start(bf16[4,2,128,128,128]{4,3,1,0,2:T(8,128)(2,1)} %copy.103), calls=%async_computation | async-start | bytes 67108864 | tf_op jit(solution)/shard_map/all_to_all | solution.py:24
  123.7 896.0 %all-reduce.2.cloned.1.call-start = ((), (), s32[]{:S(2)}) async-start(), calls=%async_computation.1 | async-start | bytes 524288 | tf_op jit(solution)/shard_map/psum | solution.py:71
  859.7 23.1 %copy-start.4 = (f32[4,2,8,16]{3,2,1,0:T(8,128)}, f32[4,2,8,16]{3,2,1,0:T(8,128)S(1)}, u32[]{:S(2)}) copy-start(f32[4,2,8,16]{3,2,1,0:T(8,128)S(1)} %copy.105) | copy-start | bytes 12292
  978.7 3.6 copy-start.2
  982.3 2.2 copy-start.1
  983.6 2.4 copy-start
Sparse Core Ops, SparseCore 0:
  988.3 31.3 all-reduce.1
where the time goes:
time: 1030 us
  waiting for transfers between devices  755 us (73%)
  local copies, waits for them, and re-layouts  171 us (17%)
  other arithmetic  39.3 us (4%)
  matrix products  21.1 us (2%)
  blocking collectives  20.4 us (2%)
  between operations  14.3 us (1%)
    all_to_all x1, waiting for transfers between devices, on_device(): lax.all_to_all(arranged, 'blk', split_axis=2, concat_axis=3, tiled=True)  723 us
    unnamed x25, local copies, waits for them, and re-layouts  45.2 us
    transpose x1, local copies, waits for them, and re-layouts, on_device(): kv_cache.reshape(layers, 2, batch, local_rows, heads, HEAD_DIM)  42.3 us
    psum x1, waiting for transfers between devices, on_device(): lax.psum((total * scale_factor, weighted * scale_factor[..., None]), 'seq')  31.2 us
    convert_element_type x1, other arithmetic, on_device(): (grouped.astype(jnp.float32) / block_scale[..., None, None]).astype(jnp.b...  23.3 us
    all_to_all x1, local copies, waits for them, and re-layouts, on_device(): lax.all_to_all(arranged, 'blk', split_axis=2, concat_axis=3, tiled=True)  23 us
    reshape x1, local copies, waits for them, and re-layouts, on_device(): arranged = arranged.reshape(layers, 2, heads * batch, local_rows, HEAD_DIM)  22.9 us
    convert_element_type x1, local copies, waits for them, and re-layouts, on_device(): (grouped.astype(jnp.float32) / block_scale[..., None, None]).astype(jnp.b...  22.9 us
  transfers between devices with their start and end apart: 2, of which 2 were waited for; matrix products, arithmetic and copies ran while one was open for 0% of the time, Pallas kernels for 0%

commit v1 on v0

--- a/solution.py
+++ b/solution.py
@@ -1,14 +1,337 @@
+import functools
+import math
+
 import jax
 import jax.numpy as jnp
 from jax import lax
+from jax.experimental import pallas as pl
+from jax.experimental.pallas import tpu as pltpu
 from jax.sharding import PartitionSpec as P
 
 HEAD_DIM = 128
 QUERY_GROUP = 8
 BLOCK = 128
-
-
-def on_device(kv_cache, queries, fresh_key_value, lengths):
+NEG = -1e30
+
+
+def partner(me, step, count):
+    if count & (count - 1) == 0:
+        return me ^ step
+    return (me + step) % count
+
+
+def source(me, step, count):
+    if count & (count - 1) == 0:
+        return me ^ step
+    return (me + count - step) % count
+
+
+def cost(flops, nbytes):
+    return pl.CostEstimate(flops=flops, bytes_accessed=nbytes, transcendentals=0)
+
+
+def params(**kw):
+    return pltpu.CompilerParams(vmem_limit_bytes=40 * 2**20, **kw)
+
+
+def prep_kernel(place, *refs):
+    half = len(refs) // 2
+    for src, dst in zip(refs[:half], refs[half:]):
+        dst[...] = src[0, 0]
+
+
+def prepare(kv_cache, place, layer, which, low, number, count):
+    _, _, batch, rows, width = kv_cache.shape
+    pairs = width // HEAD_DIM * batch // count
+    per = math.gcd(number, low, batch, 4)
+
+    def where(step):
+        def index(i, place):
+            peer = partner(place[0], step, count)
+            first = peer * pairs + low + i * per
+            return (layer, which, (first % batch) // per, 0, first // batch)
+
+        return index
+
+    steps = range(1, count)
+    piece = jax.ShapeDtypeStruct((number, rows, HEAD_DIM), kv_cache.dtype)
+    return pl.pallas_call(
+        prep_kernel,
+        grid_spec=pltpu.PrefetchScalarGridSpec(
+            num_scalar_prefetch=1,
+            grid=(number // per,),
+            in_specs=[pl.BlockSpec((1, 1, per, rows, HEAD_DIM), where(s)) for s in steps],
+            out_specs=[pl.BlockSpec((per, rows, HEAD_DIM), lambda i, place: (i, 0, 0)) for s in steps],
+        ),
+        out_shape=[piece for _ in steps],
+        cost_estimate=cost(10**7, 4 * number * rows * HEAD_DIM * count),
+        compiler_params=params(),
+        name="prepare",
+    )(place, *[kv_cache for _ in steps])
+
+
+def gather_pair(place, pieces, raw, j, rows, count):
+    for step, piece in enumerate(pieces):
+        at = source(place[0], step, count) * rows
+        values = piece[0, 0, j] if step == 0 else piece[j]
+        raw[pl.ds(pl.multiple_of(at, rows), rows), :] = values
+
+
+def quantize(raw, out, j, n):
+    at = pl.ds(n * BLOCK, BLOCK)
+    values = raw[at, :].astype(jnp.float32)
+    high = jnp.maximum(jnp.max(jnp.abs(values), axis=(0, 1), keepdims=True), 1.0)
+    quant = (values * (127.0 / high)).astype(jnp.bfloat16)
+    out[0, 0, j, at, :] = quant
+    return high / 127.0, quant
+
+
+def key_kernel(low, batch, blocks, count, place, lengths, own, *refs):
+    pieces = (own,) + refs[: count - 1]
+    query = refs[count - 1]
+    quant_out, scale_out, weight_out, stat_out, summary_out, raw = refs[-6:]
+    per, rows = own.shape[2], own.shape[3]
+    pairs = scale_out.shape[2]
+    step = pl.program_id(0)
+    lane = lax.broadcasted_iota(jnp.int32, (QUERY_GROUP, BLOCK), 1)
+    inverse = 1.0 / math.sqrt(HEAD_DIM)
+    for j in range(per):
+        gather_pair(place, pieces, raw.at[j], j, rows, count)
+        pair = low + step * per + j
+        live = lengths[(place[0] * pairs + pair) % batch] - place[1] * (rows * count)
+        scales = jnp.zeros((1, BLOCK), jnp.float32)
+        peaks = jnp.full((QUERY_GROUP, BLOCK), NEG, jnp.float32)
+        totals = jnp.zeros((QUERY_GROUP, BLOCK), jnp.float32)
+        for n in range(blocks):
+            scale, quant = quantize(raw.at[j], quant_out, j, n)
+            scales = jnp.where(lane[:1] == n, scale, scales)
+            score = lax.dot_general(
+                query[0, j], quant, (((1,), (1,)), ((), ())), preferred_element_type=jnp.float32
+            )
+            valid = lane + n * BLOCK < live
+            masked = jnp.where(valid, score * scale * inverse, NEG)
+            peak = jnp.max(masked, axis=1, keepdims=True)
+            weight = jnp.where(valid, jnp.exp(masked - peak), 0.0)
+            weight_out[j, :, pl.ds(n * BLOCK, BLOCK)] = weight
+            peaks = jnp.where(lane == n, peak, peaks)
+            totals = jnp.where(lane == n, jnp.sum(weight, axis=1, keepdims=True), totals)
+        scale_out[0, 0, pl.ds(pair, 1), :] = scales[:, :blocks]
+        stat_out[j] = peaks
+        top = jnp.max(peaks, axis=1, keepdims=True)
+        total = jnp.sum(jnp.exp(peaks - top) * totals, axis=1, keepdims=True)
+        summary_out[j] = jnp.where(lane == 0, top, total)
+
+
+def value_kernel(low, batch, blocks, count, place, lengths, own, *refs):
+    pieces = (own,) + refs[: count - 1]
+    weight_in, stat_in, plan_in = refs[count - 1 : count + 2]
+    quant_out, scale_out, sum_out, raw = refs[-4:]
+    per, rows = own.shape[2], own.shape[3]
+    step = pl.program_id(0)
+    lane = lax.broadcasted_iota(jnp.int32, (1, BLOCK), 1)
+    for j in range(per):
+        gather_pair(place, pieces, raw.at[j], j, rows, count)
+        pair = low + step * per + j
+        scales = jnp.zeros((1, BLOCK), jnp.float32)
+        factor = jnp.exp(stat_in[j] - plan_in[j, :, :1]) / plan_in[j, :, 1:2]
+        numer = jnp.zeros((QUERY_GROUP, HEAD_DIM), jnp.float32)
+        for n in range(blocks):
+            scale, quant = quantize(raw.at[j], quant_out, j, n)
+            scales = jnp.where(lane == n, scale, scales)
+            weight = (weight_in[j, :, pl.ds(n * BLOCK, BLOCK)] * scale).astype(jnp.bfloat16)
+            part = jnp.dot(weight, quant, preferred_element_type=jnp.float32)
+            numer = numer + factor[:, n : n + 1] * part
+        scale_out[0, 0, pl.ds(pair, 1), :] = scales[:, :blocks]
+        sum_out[j] = numer
+
+
+def consume(kernel, kv_cache, pieces, place, lengths, extra, outs, held, layer, which, low, number, count):
+    layers, _, batch, rows, width = kv_cache.shape
+    pairs = width // HEAD_DIM * batch // count
+    seq_rows = rows * count
+    blocks = seq_rows // BLOCK
+    per = math.gcd(number, low, 2)
+
+    def mine(i, place, lengths):
+        first = place[0] * pairs + low + i * per
+        return (layer, which, (first % batch) // per, 0, first // batch)
+
+    def big(i, place, lengths):
+        return (layer, which, low // per + i, 0, 0)
+
+    def rest(shape, layered):
+        if layered:
+            return pl.BlockSpec((1, per, *shape[2:]), lambda i, a, b: (layer, low // per + i, *[0] * (len(shape) - 2)))
+        return pl.BlockSpec((per, *shape[1:]), lambda i, a, b: (low // per + i, *[0] * (len(shape) - 1)))
+
+    in_specs = [pl.BlockSpec((1, 1, per, rows, HEAD_DIM), mine)]
+    in_specs += [pl.BlockSpec((per, rows, HEAD_DIM), lambda i, place, lengths: (i, 0, 0)) for _ in pieces]
+    in_specs += [rest(x.shape, x.ndim == 4) for x in extra]
+    operands = [kv_cache, *pieces, *extra]
+    aliases = {}
+    for at, array in enumerate(held):
+        if array is not None:
+            aliases[2 + len(operands)] = at
+            in_specs.append(pl.BlockSpec(memory_space=pl.ANY))
+            operands.append(array)
+    return pl.pallas_call(
+        functools.partial(kernel, low, batch, blocks, count),
+        grid_spec=pltpu.PrefetchScalarGridSpec(
+            num_scalar_prefetch=2,
+            grid=(number // per,),
+            in_specs=in_specs,
+            out_specs=[
+                pl.BlockSpec((1, 1, per, seq_rows, HEAD_DIM), big),
+                pl.BlockSpec((1, 1, pairs, blocks), lambda i, place, lengths: (layer, which, 0, 0)),
+                *[rest(x.shape, False) for x in outs],
+            ],
+            scratch_shapes=[pltpu.VMEM((per, seq_rows, HEAD_DIM), jnp.bfloat16)],
+        ),
+        out_shape=[
+            jax.ShapeDtypeStruct((layers, 2, pairs, seq_rows, HEAD_DIM), jnp.bfloat16),
+            jax.ShapeDtypeStruct((layers, 2, pairs, blocks), jnp.float32),
+            *outs,
+        ],
+        input_output_aliases=aliases,
+        cost_estimate=cost(10**7, 4 * number * seq_rows * HEAD_DIM),
+        compiler_params=params(),
+    )(place, lengths, *operands)
+
+
+def tree(join, values):
+    while len(values) > 1:
+        values = [join(*values[i : i + 2]) if i + 1 < len(values) else values[i] for i in range(0, len(values), 2)]
+    return values[0]
+
+
+def plan_kernel(query, fresh, *refs):
+    summaries, plan_out, term_out = refs[:-2], refs[-2], refs[-1]
+    lane = lax.broadcasted_iota(jnp.int32, (1, 1, BLOCK), 2)
+    own = jnp.sum(
+        query[0].astype(jnp.float32) * fresh[0, 0].astype(jnp.float32)[:, None, :], axis=-1, keepdims=True
+    ) * (1.0 / math.sqrt(HEAD_DIM))
+    top = jnp.maximum(tree(jnp.maximum, [s[:, :, :1] for s in summaries]), own)
+    own_weight = jnp.exp(own - top)
+    denom = tree(jnp.add, [jnp.exp(s[:, :, :1] - top) * s[:, :, 1:2] for s in summaries]) + own_weight
+    plan_out[...] = jnp.where(lane == 0, top, denom)
+    term_out[...] = own_weight / denom * fresh[0, 1].astype(jnp.float32)[:, None, :]
+
+
+def make_plan(grouped, fresh, summaries, layer):
+    pairs = grouped.shape[1]
+    shape = (pairs, QUERY_GROUP, HEAD_DIM)
+    whole = pl.BlockSpec(shape, lambda i: (0, 0, 0))
+    return pl.pallas_call(
+        plan_kernel,
+        grid=(1,),
+        in_specs=[
+            pl.BlockSpec((1, *shape), lambda i: (layer, 0, 0, 0)),
+            pl.BlockSpec((1, 2, pairs, HEAD_DIM), lambda i: (layer, 0, 0, 0)),
+            *[whole for _ in summaries],
+        ],
+        out_specs=[whole, whole],
+        out_shape=[jax.ShapeDtypeStruct(shape, jnp.float32)] * 2,
+        cost_estimate=cost(10**6, 10**6),
+        compiler_params=params(),
+        name="plan",
+    )(grouped, fresh, *summaries)
+
+
+def finish_kernel(members, term, *refs):
+    out = refs[-1]
+    result = tree(jnp.add, [s[...] for s in refs[:members]]) + term[...]
+    for g in range(QUERY_GROUP):
+        out[0, :, g * HEAD_DIM : (g + 1) * HEAD_DIM] = result[:, g, :].astype(jnp.bfloat16)
+
+
+def finish(term, shares, held, layer, layers):
+    pairs = term.shape[0]
+    width = QUERY_GROUP * HEAD_DIM
+    whole = pl.BlockSpec(term.shape, lambda i: (0, 0, 0))
+    operands = [term, *shares]
+    in_specs = [whole for _ in operands]
+    aliases = {}
+    if held is not None:
+        aliases = {len(operands): 0}
+        in_specs.append(pl.BlockSpec(memory_space=pl.ANY))
+        operands.append(held)
+    return pl.pallas_call(
+        functools.partial(finish_kernel, len(shares)),
+        grid=(1,),
+        in_specs=in_specs,
+        out_specs=pl.BlockSpec((1, pairs, width), lambda i: (layer, 0, 0)),
+        out_shape=jax.ShapeDtypeStruct((layers, pairs, width), jnp.bfloat16),
+        input_output_aliases=aliases,
+        cost_estimate=cost(10**6, 10**6),
+        compiler_params=params(),
+        name="finish",
+    )(*operands)
+
+
+def chunks_of(layers, pairs):
+    chunks = [(layer, which, 0, pairs) for layer in range(layers) for which in (0, 1)]
+    if pairs % 16 == 0:
+        quarter = pairs // 4
+        chunks[-1:] = [
+            (layers - 1, 1, 0, 2 * quarter),
+            (layers - 1, 1, 2 * quarter, quarter),
+            (layers - 1, 1, 3 * quarter, quarter),
+        ]
+    return chunks
+
+
+def by_pieces(kv_cache, queries, fresh, lengths):
+    layers, _, batch, rows, width = kv_cache.shape
+    count = lax.axis_size("blk")
+    members = lax.axis_size("seq")
+    pairs = width // HEAD_DIM * batch // count
+    seq_rows = rows * count
+    place = jnp.stack([lax.axis_index("blk"), lax.axis_index("seq")]).astype(jnp.int32)
+    grouped = queries.reshape(layers, pairs, QUERY_GROUP, HEAD_DIM)
+    small = jax.ShapeDtypeStruct((pairs, QUERY_GROUP, HEAD_DIM), jnp.float32)
+    weight_shape = jax.ShapeDtypeStruct((pairs, QUERY_GROUP, seq_rows), jnp.float32)
+
+    def share(array):
+        shared = [array]
+        for step in range(1, members):
+            ring = [(me, partner(me, step, members)) for me in range(members)]
+            shared.append(lax.ppermute(array, "seq", ring))
+        return shared
+
+    held = [None, None]
+    attended = None
+    for layer, which, low, number in chunks_of(layers, pairs):
+        sent = prepare(kv_cache, place, layer, which, low, number, count)
+        pieces = [None] * (count - 1)
+        for step in range(1, count):
+            ring = [(me, partner(me, step, count)) for me in range(count)]
+            pieces[step - 1] = lax.ppermute(sent[step - 1], "blk", ring)
+        common = (kv_cache, pieces, place, lengths)
+        chunk = (layer, which, low, number, count)
+        last = low + number == pairs
+        if which == 0:
+            inner = [None] * 3 if low == 0 else inner
+            results = consume(
+                key_kernel, *common, (grouped,), (weight_shape, small, small), held + inner, *chunk
+            )
+            held, inner = list(results[:2]), list(results[2:])
+            if last:
+                weights, stats, summary = inner
+                summaries = share(summary)
+                plan, term = make_plan(grouped, fresh, summaries, layer)
+            continue
+        inner = [None] if low == 0 else inner
+        results = consume(
+            value_kernel, *common, (weights, stats, plan), (small,), held + inner, *chunk
+        )
+        held, inner = list(results[:2]), list(results[2:])
+        if last:
+            shares = share(inner[0])
+            attended = finish(term, shares, attended, layer, layers)
+    return (*held, attended)
+
+
+def by_all_to_all(kv_cache, queries, fresh_key_value, lengths):
     layers, _, batch, local_rows, width = kv_cache.shape
     heads = width // HEAD_DIM
     blk_count = lax.axis_size("blk")
@@ -95,6 +418,15 @@
     return (quant, block_scale, attended)
 
 
+def on_device(kv_cache, queries, fresh_key_value, lengths):
+    exchange = by_pieces if by_blocks(kv_cache.shape[3]) else by_all_to_all
+    return exchange(kv_cache, queries, fresh_key_value, lengths)
+
+
+def by_blocks(local_rows):
+    return local_rows % BLOCK == 0
+
+
 def solution(mesh):
     in_specs = (
         P(None, None, None, ("seq", "blk"), None),
@@ -107,6 +439,11 @@
         P(None, None, "blk", "seq"),
         P(None, "blk", None),
     )
-    return jax.shard_map(
-        on_device, mesh=mesh, in_specs=in_specs, out_specs=out_specs, check_vma=False
-    )
+
+    def program(kv_cache, queries, fresh_key_value, lengths):
+        step = jax.shard_map(
+            on_device, mesh=mesh, in_specs=in_specs, out_specs=out_specs, check_vma=False
+        )
+        return step(kv_cache, queries, fresh_key_value, lengths)
+
+    return program

time: 1030 us -> 798 us (0.77); the launches traced: 1030 us -> 785 us
  waiting for transfers between devices: 755 us -> 354 us
  starting transfers between devices: 7.46 us -> 291 us
  local copies, waits for them, and re-layouts: 171 us -> 30.1 us
  Pallas kernels: 0 us -> 108 us
  other arithmetic: 39.3 us -> 0.08 us
  matrix products: 21.1 us -> 0 us
  blocking collectives: 20.4 us -> 0 us
  between operations: 14.3 us -> 1.71 us
    all_to_all x1 -> x0, waiting for transfers between devices: 723 us -> none  [on_device(): lax.all_to_all(arranged, 'blk', split_axis=2, concat_axis=3, tiled=True)]
    ppermute x0 -> x94, waiting for transfers between devices: none -> 354 us  [the longest x70 350 us: by_pieces(): pieces[step - 1] = lax.ppermute(sent[step - 1], 'blk', ring)]
    ppermute x0 -> x94, starting transfers between devices: none -> 291 us  [the longest x70 275 us: by_pieces(): pieces[step - 1] = lax.ppermute(sent[step - 1], 'blk', ring)]
    pallas_call x0 -> x28, Pallas kernels: none -> 108 us  [the longest x10 68.4 us: consume(): pl.pallas_call(functools.partial(kernel, low, batch, blocks, count), grid...]
    transpose x1 -> x0, local copies, waits for them, and re-layouts: 42.3 us -> none  [on_device(): kv_cache.reshape(layers, 2, batch, local_rows, heads, HEAD_DIM)]
    psum x1 -> x0, waiting for transfers between devices: 31.2 us -> none  [on_device(): lax.psum((total * scale_factor, weighted * scale_factor[..., None]), 'seq')]
    convert_element_type x3 -> x0, other arithmetic: 24.5 us -> none  [the longest x1 23.3 us: on_device(): (grouped.astype(jnp.float32) / block_scale[..., None, None]).astype(jnp.b...]
    convert_element_type x2 -> x0, local copies, waits for them, and re-layouts: 23.6 us -> none  [the longest x1 22.9 us: on_device(): (grouped.astype(jnp.float32) / block_scale[..., None, None]).astype(jnp.b...]
  transfers between devices with their start and end apart: 2 -> 94, of which waited for: 2 -> 23; matrix products, arithmetic and copies ran while one was open for 0% -> 0% of each run, Pallas kernels for 0% -> 13%
where the time goes in v1:
time: 798 us; the launch traced here: 785 us
  waiting for transfers between devices  354 us (44%)
  starting transfers between devices  291 us (36%)
  Pallas kernels  108 us (14%)
  local copies, waits for them, and re-layouts  30.1 us (4%)
    ppermute x70, waiting for transfers between devices, by_pieces(): pieces[step - 1] = lax.ppermute(sent[step - 1], 'blk', ring)  350 us
    ppermute x70, starting transfers between devices, by_pieces(): pieces[step - 1] = lax.ppermute(sent[step - 1], 'blk', ring)  275 us
    pallas_call x10, Pallas kernels, consume(): pl.pallas_call(functools.partial(kernel, low, batch, blocks, count), grid...  68.4 us
    pallas_call x10, Pallas kernels, prepare(): pl.pallas_call(prep_kernel, grid_spec=pltpu.PrefetchScalarGridSpec(num_sc...  36 us
    unnamed x192, local copies, waits for them, and re-layouts  30.1 us
  transfers between devices with their start and end apart: 94, of which 23 were waited for; matrix products, arithmetic and copies ran while one was open for 0% of the time, Pallas kernels for 13%

profile of v1, /device:TPU:0, one launch (start us, length us, event | category | flops | bytes accessed | tf_op | source)
XLA Modules:
  0.0 784.9 jit_solution(13315492912819528843)
XLA Ops:
  2.6 3.0 collective-permute-start.68
  7.2 3.0 collective-permute-start.71
  14.1 3.6 collective-permute-start.73
  19.0 2.5 collective-permute-start
  22.1 5.0 collective-permute-start.1
  27.1 2.6 collective-permute-done.72.refs_4_
  31.4 3.8 collective-permute-start.3
  35.9 3.7 collective-permute-start.4
  40.6 4.4 collective-permute-start.6
  45.1 2.7 prepare.19
  48.9 4.2 prepare.17
  61.3 31.2 %collective-permute-done.76.refs_1_ = bf16[8,128,128]{2,1,0:T(8,128)(2,1)S(1)} collective-permute-done((bf16[8,128,128]{2,1,0:T(8,128)(2,1)S(1)}, bf16[8,128,128]{2,1,0:T(8,128)(2,1)S(1)}, u32[]{:S(2)}, u32[]{:S(2)}) %collective-permute-start.76) | collective-permute-done | bytes 262176 | tf_op jit(solution)/shard_map/ppermute | solution.py:308
  95.3 4.2 prepare.16
  102.6 3.0 collective-permute-start.55
  108.0 30.9 %collective-permute-done.53.refs_4_ = bf16[16,128,128]{2,1,0:T(8,128)(2,1)S(1)} collective-permute-done((bf16[16,128,128]{2,1,0:T(8,128)(2,1)S(1)}, bf16[16,128,128]{2,1,0:T(8,128)(2,1)S(1)}, u32[]{:S(2)}, u32[]{:S(2)}) %collective-permute-start.53) | collective-permute-done | bytes 524320 | tf_op jit(solution)/shard_map/ppermute | solution.py:308
  140.9 11.6 %collective-permute-start.45 = (bf16[16,128,128]{2,1,0:T(8,128)(2,1)S(1)}, bf16[16,128,128]{2,1,0:T(8,128)(2,1)S(1)}, u32[]{:S(2)}, u32[]{:S(2)}) collective-permute-start(bf16[16,128,128]{2,1,0:T(8,128)(2,1)S(1)} %get-tuple-element.164), channel_id=1, source_target_pairs={{0,4},{1,5},{2,6},{3,7},{4,0},{5,1},{6,2},{7,3},{8,12},{9,13},{10,... | collective-permute-start | bytes 1572872 | tf_op jit(solution)/shard_map/ppermute | solution.py:308
  153.3 24.6 %collective-permute-start.46 = (bf16[16,128,128]{2,1,0:T(8,128)(2,1)S(1)}, bf16[16,128,128]{2,1,0:T(8,128)(2,1)S(1)}, u32[]{:S(2)}, u32[]{:S(2)}) collective-permute-start(bf16[16,128,128]{2,1,0:T(8,128)(2,1)S(1)} %get-tuple-element.165), channel_id=1, source_target_pairs={{0,5},{1,4},{2,7},{3,6},{4,1},{5,0},{6,3},{7,2},{8,13},{9,12},{10,... | collective-permute-start | bytes 1572872 | tf_op jit(solution)/shard_map/ppermute | solution.py:308
  178.7 2.1 collective-permute-start.47
  183.8 4.2 prepare.15
  189.1 31.2 %collective-permute-done.45.refs_3_ = bf16[16,128,128]{2,1,0:T(8,128)(2,1)S(1)} collective-permute-done((bf16[16,128,128]{2,1,0:T(8,128)(2,1)S(1)}, bf16[16,128,128]{2,1,0:T(8,128)(2,1)S(1)}, u32[]{:S(2)}, u32[]{:S(2)}) %collective-permute-start.45) | collective-permute-done | bytes 524320 | tf_op jit(solution)/shard_map/ppermute | solution.py:308
  220.4 11.2 %collective-permute-done.46.refs_4_ = bf16[16,128,128]{2,1,0:T(8,128)(2,1)S(1)} collective-permute-done((bf16[16,128,128]{2,1,0:T(8,128)(2,1)S(1)}, bf16[16,128,128]{2,1,0:T(8,128)(2,1)S(1)}, u32[]{:S(2)}, u32[]{:S(2)}) %collective-permute-start.46) | collective-permute-done | bytes 524320 | tf_op jit(solution)/shard_map/ppermute | solution.py:308
  231.6 12.1 %collective-permute-start.38 = (bf16[16,128,128]{2,1,0:T(8,128)(2,1)S(1)}, bf16[16,128,128]{2,1,0:T(8,128)(2,1)S(1)}, u32[]{:S(2)}, u32[]{:S(2)}) collective-permute-start(bf16[16,128,128]{2,1,0:T(8,128)(2,1)S(1)} %get-tuple-element.157), channel_id=1, source_target_pairs={{0,4},{1,5},{2,6},{3,7},{4,0},{5,1},{6,2},{7,3},{8,12},{9,13},{10,... | collective-permute-start | bytes 1572872 | tf_op jit(solution)/shard_map/ppermute | solution.py:308
  243.7 24.6 %collective-permute-start.39 = (bf16[16,128,128]{2,1,0:T(8,128)(2,1)S(1)}, bf16[16,128,128]{2,1,0:T(8,128)(2,1)S(1)}, u32[]{:S(2)}, u32[]{:S(2)}) collective-permute-start(bf16[16,128,128]{2,1,0:T(8,128)(2,1)S(1)} %get-tuple-element.158), channel_id=1, source_target_pairs={{0,5},{1,4},{2,7},{3,6},{4,1},{5,0},{6,3},{7,2},{8,13},{9,12},{10,... | collective-permute-start | bytes 1572872 | tf_op jit(solution)/shard_map/ppermute | solution.py:308
  269.1 2.3 collective-permute-start.40
  271.4 4.2 prepare.14
  280.4 31.3 %collective-permute-done.38.refs_3_ = bf16[16,128,128]{2,1,0:T(8,128)(2,1)S(1)} collective-permute-done((bf16[16,128,128]{2,1,0:T(8,128)(2,1)S(1)}, bf16[16,128,128]{2,1,0:T(8,128)(2,1)S(1)}, u32[]{:S(2)}, u32[]{:S(2)}) %collective-permute-start.38) | collective-permute-done | bytes 524320 | tf_op jit(solution)/shard_map/ppermute | solution.py:308
  312.5 10.7 %collective-permute-done.39.refs_4_ = bf16[16,128,128]{2,1,0:T(8,128)(2,1)S(1)} collective-permute-done((bf16[16,128,128]{2,1,0:T(8,128)(2,1)S(1)}, bf16[16,128,128]{2,1,0:T(8,128)(2,1)S(1)}, u32[]{:S(2)}, u32[]{:S(2)}) %collective-permute-start.39) | collective-permute-done | bytes 524320 | tf_op jit(solution)/shard_map/ppermute | solution.py:308
  324.9 10.8 %collective-permute-start.31 = (bf16[16,128,128]{2,1,0:T(8,128)(2,1)S(1)}, bf16[16,128,128]{2,1,0:T(8,128)(2,1)S(1)}, u32[]{:S(2)}, u32[]{:S(2)}) collective-permute-start(bf16[16,128,128]{2,1,0:T(8,128)(2,1)S(1)} %get-tuple-element.150), channel_id=1, source_target_pairs={{0,4},{1,5},{2,6},{3,7},{4,0},{5,1},{6,2},{7,3},{8,12},{9,13},{10,... | collective-permute-start | bytes 1572872 | tf_op jit(solution)/shard_map/ppermute | solution.py:308
  336.4 24.3 %collective-permute-start.32 = (bf16[16,128,128]{2,1,0:T(8,128)(2,1)S(1)}, bf16[16,128,128]{2,1,0:T(8,128)(2,1)S(1)}, u32[]{:S(2)}, u32[]{:S(2)}) collective-permute-start(bf16[16,128,128]{2,1,0:T(8,128)(2,1)S(1)} %get-tuple-element.151), channel_id=1, source_target_pairs={{0,5},{1,4},{2,7},{3,6},{4,1},{5,0},{6,3},{7,2},{8,13},{9,12},{10,... | collective-permute-start | bytes 1572872 | tf_op jit(solution)/shard_map/ppermute | solution.py:308
  361.5 2.8 collective-permute-start.33
  366.6 4.2 prepare.13
  371.9 31.9 %collective-permute-done.31.refs_3_ = bf16[16,128,128]{2,1,0:T(8,128)(2,1)S(1)} collective-permute-done((bf16[16,128,128]{2,1,0:T(8,128)(2,1)S(1)}, bf16[16,128,128]{2,1,0:T(8,128)(2,1)S(1)}, u32[]{:S(2)}, u32[]{:S(2)}) %collective-permute-start.31) | collective-permute-done | bytes 524320 | tf_op jit(solution)/shard_map/ppermute | solution.py:308
  404.6 10.8 %collective-permute-done.32.refs_4_ = bf16[16,128,128]{2,1,0:T(8,128)(2,1)S(1)} collective-permute-done((bf16[16,128,128]{2,1,0:T(8,128)(2,1)S(1)}, bf16[16,128,128]{2,1,0:T(8,128)(2,1)S(1)}, u32[]{:S(2)}, u32[]{:S(2)}) %collective-permute-start.32) | collective-permute-done | bytes 524320 | tf_op jit(solution)/shard_map/ppermute | solution.py:308
  417.1 10.2 %collective-permute-start.24 = (bf16[16,128,128]{2,1,0:T(8,128)(2,1)S(1)}, bf16[16,128,128]{2,1,0:T(8,128)(2,1)S(1)}, u32[]{:S(2)}, u32[]{:S(2)}) collective-permute-start(bf16[16,128,128]{2,1,0:T(8,128)(2,1)S(1)} %get-tuple-element.143), channel_id=1, source_target_pairs={{0,4},{1,5},{2,6},{3,7},{4,0},{5,1},{6,2},{7,3},{8,12},{9,13},{10,... | collective-permute-start | bytes 1572872 | tf_op jit(solution)/shard_map/ppermute | solution.py:308
  428.1 24.2 %collective-permute-start.25 = (bf16[16,128,128]{2,1,0:T(8,128)(2,1)S(1)}, bf16[16,128,128]{2,1,0:T(8,128)(2,1)S(1)}, u32[]{:S(2)}, u32[]{:S(2)}) collective-permute-start(bf16[16,128,128]{2,1,0:T(8,128)(2,1)S(1)} %get-tuple-element.144), channel_id=1, source_target_pairs={{0,5},{1,4},{2,7},{3,6},{4,1},{5,0},{6,3},{7,2},{8,13},{9,12},{10,... | collective-permute-start | bytes 1572872 | tf_op jit(solution)/shard_map/ppermute | solution.py:308
  453.1 3.0 collective-permute-start.26
  458.3 4.2 prepare.12
  463.6 32.0 %collective-permute-done.24.refs_3_ = bf16[16,128,128]{2,1,0:T(8,128)(2,1)S(1)} collective-permute-done((bf16[16,128,128]{2,1,0:T(8,128)(2,1)S(1)}, bf16[16,128,128]{2,1,0:T(8,128)(2,1)S(1)}, u32[]{:S(2)}, u32[]{:S(2)}) %collective-permute-start.24) | collective-permute-done | bytes 524320 | tf_op jit(solution)/shard_map/ppermute | solution.py:308
  495.7 11.6 %collective-permute-done.25.refs_4_ = bf16[16,128,128]{2,1,0:T(8,128)(2,1)S(1)} collective-permute-done((bf16[16,128,128]{2,1,0:T(8,128)(2,1)S(1)}, bf16[16,128,128]{2,1,0:T(8,128)(2,1)S(1)}, u32[]{:S(2)}, u32[]{:S(2)}) %collective-permute-start.25) | collective-permute-done | bytes 524320 | tf_op jit(solution)/shard_map/ppermute | solution.py:308
  507.3 10.7 %collective-permute-start.17 = (bf16[16,128,128]{2,1,0:T(8,128)(2,1)S(1)}, bf16[16,128,128]{2,1,0:T(8,128)(2,1)S(1)}, u32[]{:S(2)}, u32[]{:S(2)}) collective-permute-start(bf16[16,128,128]{2,1,0:T(8,128)(2,1)S(1)} %get-tuple-element.136), channel_id=1, source_target_pairs={{0,4},{1,5},{2,6},{3,7},{4,0},{5,1},{6,2},{7,3},{8,12},{9,13},{10,... | collective-permute-start | bytes 1572872 | tf_op jit(solution)/shard_map/ppermute | solution.py:308
  518.2 8.3 %shard_map.67 = (bf16[4,2,16,1024,128]{4,3,2,1,0:T(8,128)(2,1)}, f32[4,2,16,8]{3,2,1,0:T(8,128)S(1)}, f32[16,8,1024]{2,1,0:T(8,128)S(1)}, f32[16,8,128]{2,1,0:T(8,128)S(1)}, f32[16,8,128]{2,1,0:T(8,128)S(1)}) custom-call(s32[2]{0:T(128)S(1)} %pad_add_fusion.place, s32[16]{0:T(128)S(1)} %copy-done.93, bf16[4,2,16,128,1024]{4,3,2,1,0:T(8,128)(2,1)} %own.19, ...), custom_call_target="tpu_custom_call" | custom-call | flops 10000000 | bytes 8388608 | tf_op jit(solution)/shard_map/pallas_call | solution.py:177
  528.6 16.0 %collective-permute-start.18 = (bf16[16,128,128]{2,1,0:T(8,128)(2,1)S(1)}, bf16[16,128,128]{2,1,0:T(8,128)(2,1)S(1)}, u32[]{:S(2)}, u32[]{:S(2)}) collective-permute-start(bf16[16,128,128]{2,1,0:T(8,128)(2,1)S(1)} %get-tuple-element.137), channel_id=1, source_target_pairs={{0,5},{1,4},{2,7},{3,6},{4,1},{5,0},{6,3},{7,2},{8,13},{9,12},{10,... | collective-permute-start | bytes 1572872 | tf_op jit(solution)/shard_map/ppermute | solution.py:308
  544.7 4.2 prepare.11
  548.9 15.1 %collective-permute-done.17.refs_3_ = bf16[16,128,128]{2,1,0:T(8,128)(2,1)S(1)} collective-permute-done((bf16[16,128,128]{2,1,0:T(8,128)(2,1)S(1)}, bf16[16,128,128]{2,1,0:T(8,128)(2,1)S(1)}, u32[]{:S(2)}, u32[]{:S(2)}) %collective-permute-start.17) | collective-permute-done | bytes 524320 | tf_op jit(solution)/shard_map/ppermute | solution.py:308
  565.2 3.0 collective-permute-start.20
  568.1 3.5 collective-permute-start.11
  572.1 7.8 shard_map.68
  580.0 9.0 %shard_map.69 = (bf16[4,2,16,1024,128]{4,3,2,1,0:T(8,128)(2,1)}, f32[4,2,16,8]{3,2,1,0:T(8,128)S(1)}, f32[16,8,1024]{2,1,0:T(8,128)S(1)}, f32[16,8,128]{2,1,0:T(8,128)S(1)}, f32[16,8,128]{2,1,0:T(8,128)S(1)}) custom-call(s32[2]{0:T(128)S(1)} %pad_add_fusion.place, s32[16]{0:T(128)S(1)} %copy-done.93, ...), custom_call_target="tpu_custom_call", output_to_operand_aliasing={{0}: (11, {}), {1}: (12, {})} | custom-call | flops 10000000 | bytes 8388608 | tf_op jit(solution)/shard_map/pallas_call | solution.py:177
  589.1 31.4 %collective-permute-done.18.refs_4_ = bf16[16,128,128]{2,1,0:T(8,128)(2,1)S(1)} collective-permute-done((bf16[16,128,128]{2,1,0:T(8,128)(2,1)S(1)}, bf16[16,128,128]{2,1,0:T(8,128)(2,1)S(1)}, u32[]{:S(2)}, u32[]{:S(2)}) %collective-permute-start.18) | collective-permute-done | bytes 524320 | tf_op jit(solution)/shard_map/ppermute | solution.py:308
  622.4 31.5 %collective-permute-done.10.refs_3_ = bf16[16,128,128]{2,1,0:T(8,128)(2,1)S(1)} collective-permute-done((bf16[16,128,128]{2,1,0:T(8,128)(2,1)S(1)}, bf16[16,128,128]{2,1,0:T(8,128)(2,1)S(1)}, u32[]{:S(2)}, u32[]{:S(2)}) %collective-permute-start.10) | collective-permute-done | bytes 524320 | tf_op jit(solution)/shard_map/ppermute | solution.py:308
  655.1 21.6 %collective-permute-done.11.refs_4_ = bf16[16,128,128]{2,1,0:T(8,128)(2,1)S(1)} collective-permute-done((bf16[16,128,128]{2,1,0:T(8,128)(2,1)S(1)}, bf16[16,128,128]{2,1,0:T(8,128)(2,1)S(1)}, u32[]{:S(2)}, u32[]{:S(2)}) %collective-permute-start.11) | collective-permute-done | bytes 524320 | tf_op jit(solution)/shard_map/ppermute | solution.py:308
  679.5 2.4 collective-permute-start.9
  682.3 7.5 shard_map.70
  689.8 8.7 %shard_map.71 = (bf16[4,2,16,1024,128]{4,3,2,1,0:T(8,128)(2,1)}, f32[4,2,16,8]{3,2,1,0:T(8,128)S(1)}, f32[16,8,1024]{2,1,0:T(8,128)S(1)}, f32[16,8,128]{2,1,0:T(8,128)S(1)}, f32[16,8,128]{2,1,0:T(8,128)S(1)}) custom-call(s32[2]{0:T(128)S(1)} %pad_add_fusion.place, s32[16]{0:T(128)S(1)} %copy-done.93, ...), custom_call_target="tpu_custom_call", output_to_operand_aliasing={{0}: (11, {}), {1}: (12, {})} | custom-call | flops 10000000 | bytes 8388608 | tf_op jit(solution)/shard_map/pallas_call | solution.py:177
  700.1 2.3 collective-permute-done.7.refs_0_
  703.4 16.0 %collective-permute-start.77 = (bf16[8,128,128]{2,1,0:T(8,128)(2,1)S(1)}, bf16[8,128,128]{2,1,0:T(8,128)(2,1)S(1)}, u32[]{:S(2)}, u32[]{:S(2)}) collective-permute-start(bf16[8,128,128]{2,1,0:T(8,128)(2,1)S(1)} %get-tuple-element.212), channel_id=1, source_target_pairs={{0,3},{1,2},{2,1},{3,0},{4,7},{5,6},{6,5},{7,4},{8,11},{9,10},{10,... | collective-permute-start | bytes 786440 | tf_op jit(solution)/shard_map/ppermute | solution.py:308
  719.5 3.0 collective-permute-start.78
  722.7 5.0 collective-permute-start.80
  728.1 7.5 shard_map.72
  735.7 8.7 %shard_map.73 = (bf16[4,2,16,1024,128]{4,3,2,1,0:T(8,128)(2,1)}, f32[4,2,16,8]{3,2,1,0:T(8,128)S(1)}, f32[16,8,1024]{2,1,0:T(8,128)S(1)}, f32[16,8,128]{2,1,0:T(8,128)S(1)}, f32[16,8,128]{2,1,0:T(8,128)S(1)}) custom-call(s32[2]{0:T(128)S(1)} %pad_add_fusion.place, s32[16]{0:T(128)S(1)} %copy-done.93, ...), custom_call_target="tpu_custom_call", output_to_operand_aliasing={{0}: (11, {}), {1}: (12, {})} | custom-call | flops 10000000 | bytes 8388608 | tf_op jit(solution)/shard_map/pallas_call | solution.py:177
  745.3 12.6 %collective-permute-done.79.refs_4_ = bf16[8,128,128]{2,1,0:T(8,128)(2,1)S(1)} collective-permute-done((bf16[8,128,128]{2,1,0:T(8,128)(2,1)S(1)}, bf16[8,128,128]{2,1,0:T(8,128)(2,1)S(1)}, u32[]{:S(2)}, u32[]{:S(2)}) %collective-permute-start.79) | collective-permute-done | bytes 262176 | tf_op jit(solution)/shard_map/ppermute | solution.py:308
  764.7 4.6 shard_map.74
  769.5 3.1 shard_map.75
  772.6 3.1 shard_map.76
  (345 shorter events, 87.9 us)
Async XLA Ops:
  31.4 21.7 %collective-permute-start.3 = (bf16[4,128,128]{2,1,0:T(8,128)(2,1)S(1)}, bf16[4,128,128]{2,1,0:T(8,128)(2,1)S(1)}, u32[]{:S(2)}, u32[]{:S(2)}) collective-permute-start(bf16[4,128,128]{2,1,0:T(8,128)(2,1)S(1)} %get-tuple-element.122), channel_id=1, source_target_pairs={{0,4},{1,5},{2,6},{3,7},{4,0},{5,1},{6,2},{7,3},{8,12},{9,13},{10,... | collective-permute-start | bytes 393224 | tf_op jit(solution)/shard_map/ppermute | solution.py:308
  53.8 45.7 %collective-permute-start.49 = (bf16[16,128,128]{2,1,0:T(8,128)(2,1)S(1)}, bf16[16,128,128]{2,1,0:T(8,128)(2,1)S(1)}, u32[]{:S(2)}, u32[]{:S(2)}) collective-permute-start(bf16[16,128,128]{2,1,0:T(8,128)(2,1)S(1)} %get-tuple-element.168), channel_id=1, source_target_pairs={{0,1},{1,0},{2,3},{3,2},{4,5},{5,4},{6,7},{7,6},{8,9},{9,8},{10,11... | collective-permute-start | bytes 1572872 | tf_op jit(solution)/shard_map/ppermute | solution.py:308
  56.0 45.8 %collective-permute-start.50 = (bf16[16,128,128]{2,1,0:T(8,128)(2,1)S(1)}, bf16[16,128,128]{2,1,0:T(8,128)(2,1)S(1)}, u32[]{:S(2)}, u32[]{:S(2)}) collective-permute-start(bf16[16,128,128]{2,1,0:T(8,128)(2,1)S(1)} %get-tuple-element.169), channel_id=1, source_target_pairs={{0,2},{1,3},{2,0},{3,1},{4,6},{5,7},{6,4},{7,5},{8,10},{9,11},{10,... | collective-permute-start | bytes 1572872 | tf_op jit(solution)/shard_map/ppermute | solution.py:308
  56.6 49.0 %collective-permute-start.51 = (bf16[16,128,128]{2,1,0:T(8,128)(2,1)S(1)}, bf16[16,128,128]{2,1,0:T(8,128)(2,1)S(1)}, u32[]{:S(2)}, u32[]{:S(2)}) collective-permute-start(bf16[16,128,128]{2,1,0:T(8,128)(2,1)S(1)} %get-tuple-element.170), channel_id=1, source_target_pairs={{0,3},{1,2},{2,1},{3,0},{4,7},{5,6},{6,5},{7,4},{8,11},{9,10},{10,... | collective-permute-start | bytes 1572872 | tf_op jit(solution)/shard_map/ppermute | solution.py:308
  59.2 48.0 %collective-permute-start.52 = (bf16[16,128,128]{2,1,0:T(8,128)(2,1)S(1)}, bf16[16,128,128]{2,1,0:T(8,128)(2,1)S(1)}, u32[]{:S(2)}, u32[]{:S(2)}) collective-permute-start(bf16[16,128,128]{2,1,0:T(8,128)(2,1)S(1)} %get-tuple-element.171), channel_id=1, source_target_pairs={{0,4},{1,5},{2,6},{3,7},{4,0},{5,1},{6,2},{7,3},{8,12},{9,13},{10,... | collective-permute-start | bytes 1572872 | tf_op jit(solution)/shard_map/ppermute | solution.py:308
  60.2 32.3 %collective-permute-start.76 = (bf16[8,128,128]{2,1,0:T(8,128)(2,1)S(1)}, bf16[8,128,128]{2,1,0:T(8,128)(2,1)S(1)}, u32[]{:S(2)}, u32[]{:S(2)}) collective-permute-start(bf16[8,128,128]{2,1,0:T(8,128)(2,1)S(1)} %get-tuple-element.211), channel_id=1, source_target_pairs={{0,2},{1,3},{2,0},{3,1},{4,6},{5,7},{6,4},{7,5},{8,10},{9,11},{10,... | collective-permute-start | bytes 786440 | tf_op jit(solution)/shard_map/ppermute | solution.py:308
  93.2 45.7 %collective-permute-start.53 = (bf16[16,128,128]{2,1,0:T(8,128)(2,1)S(1)}, bf16[16,128,128]{2,1,0:T(8,128)(2,1)S(1)}, u32[]{:S(2)}, u32[]{:S(2)}) collective-permute-start(bf16[16,128,128]{2,1,0:T(8,128)(2,1)S(1)} %get-tuple-element.172), channel_id=1, source_target_pairs={{0,5},{1,4},{2,7},{3,6},{4,1},{5,0},{6,3},{7,2},{8,13},{9,12},{10,... | collective-permute-start | bytes 1572872 | tf_op jit(solution)/shard_map/ppermute | solution.py:308
  100.3 39.8 %collective-permute-start.54 = (bf16[16,128,128]{2,1,0:T(8,128)(2,1)S(1)}, bf16[16,128,128]{2,1,0:T(8,128)(2,1)S(1)}, u32[]{:S(2)}, u32[]{:S(2)}) collective-permute-start(bf16[16,128,128]{2,1,0:T(8,128)(2,1)S(1)} %get-tuple-element.173), channel_id=1, source_target_pairs={{0,6},{1,7},{2,4},{3,5},{4,2},{5,3},{6,0},{7,1},{8,14},{9,15},{10,... | collective-permute-start | bytes 1572872 | tf_op jit(solution)/shard_map/ppermute | solution.py:308
  102.6 49.9 %collective-permute-start.55 = (bf16[16,128,128]{2,1,0:T(8,128)(2,1)S(1)}, bf16[16,128,128]{2,1,0:T(8,128)(2,1)S(1)}, u32[]{:S(2)}, u32[]{:S(2)}) collective-permute-start(bf16[16,128,128]{2,1,0:T(8,128)(2,1)S(1)} %get-tuple-element.174), channel_id=1, source_target_pairs={{0,7},{1,6},{2,5},{3,4},{4,3},{5,2},{6,1},{7,0},{8,15},{9,14},{10,... | collective-permute-start | bytes 1572872 | tf_op jit(solution)/shard_map/ppermute | solution.py:308
  106.4 71.5 %collective-permute-start.42 = (bf16[16,128,128]{2,1,0:T(8,128)(2,1)S(1)}, bf16[16,128,128]{2,1,0:T(8,128)(2,1)S(1)}, u32[]{:S(2)}, u32[]{:S(2)}) collective-permute-start(bf16[16,128,128]{2,1,0:T(8,128)(2,1)S(1)} %get-tuple-element.161), channel_id=1, source_target_pairs={{0,1},{1,0},{2,3},{3,2},{4,5},{5,4},{6,7},{7,6},{8,9},{9,8},{10,11... | collective-permute-start | bytes 1572872 | tf_op jit(solution)/shard_map/ppermute | solution.py:308
  108.0 72.8 %collective-permute-start.43 = (bf16[16,128,128]{2,1,0:T(8,128)(2,1)S(1)}, bf16[16,128,128]{2,1,0:T(8,128)(2,1)S(1)}, u32[]{:S(2)}, u32[]{:S(2)}) collective-permute-start(bf16[16,128,128]{2,1,0:T(8,128)(2,1)S(1)} %get-tuple-element.162), channel_id=1, source_target_pairs={{0,2},{1,3},{2,0},{3,1},{4,6},{5,7},{6,4},{7,5},{8,10},{9,11},{10,... | collective-permute-start | bytes 1572872 | tf_op jit(solution)/shard_map/ppermute | solution.py:308
  139.7 48.3 %collective-permute-start.44 = (bf16[16,128,128]{2,1,0:T(8,128)(2,1)S(1)}, bf16[16,128,128]{2,1,0:T(8,128)(2,1)S(1)}, u32[]{:S(2)}, u32[]{:S(2)}) collective-permute-start(bf16[16,128,128]{2,1,0:T(8,128)(2,1)S(1)} %get-tuple-element.163), channel_id=1, source_target_pairs={{0,3},{1,2},{2,1},{3,0},{4,7},{5,6},{6,5},{7,4},{8,11},{9,10},{10,... | collective-permute-start | bytes 1572872 | tf_op jit(solution)/shard_map/ppermute | solution.py:308
  140.9 79.5 %collective-permute-start.45 = (bf16[16,128,128]{2,1,0:T(8,128)(2,1)S(1)}, bf16[16,128,128]{2,1,0:T(8,128)(2,1)S(1)}, u32[]{:S(2)}, u32[]{:S(2)}) collective-permute-start(bf16[16,128,128]{2,1,0:T(8,128)(2,1)S(1)} %get-tuple-element.164), channel_id=1, source_target_pairs={{0,4},{1,5},{2,6},{3,7},{4,0},{5,1},{6,2},{7,3},{8,12},{9,13},{10,... | collective-permute-start | bytes 1572872 | tf_op jit(solution)/shard_map/ppermute | solution.py:308
  153.3 78.2 %collective-permute-start.46 = (bf16[16,128,128]{2,1,0:T(8,128)(2,1)S(1)}, bf16[16,128,128]{2,1,0:T(8,128)(2,1)S(1)}, u32[]{:S(2)}, u32[]{:S(2)}) collective-permute-start(bf16[16,128,128]{2,1,0:T(8,128)(2,1)S(1)} %get-tuple-element.165), channel_id=1, source_target_pairs={{0,5},{1,4},{2,7},{3,6},{4,1},{5,0},{6,3},{7,2},{8,13},{9,12},{10,... | collective-permute-start | bytes 1572872 | tf_op jit(solution)/shard_map/ppermute | solution.py:308
  178.7 52.8 %collective-permute-start.47 = (bf16[16,128,128]{2,1,0:T(8,128)(2,1)S(1)}, bf16[16,128,128]{2,1,0:T(8,128)(2,1)S(1)}, u32[]{:S(2)}, u32[]{:S(2)}) collective-permute-start(bf16[16,128,128]{2,1,0:T(8,128)(2,1)S(1)} %get-tuple-element.166), channel_id=1, source_target_pairs={{0,6},{1,7},{2,4},{3,5},{4,2},{5,3},{6,0},{7,1},{8,14},{9,15},{10,... | collective-permute-start | bytes 1572872 | tf_op jit(solution)/shard_map/ppermute | solution.py:308
  181.7 62.0 %collective-permute-start.48 = (bf16[16,128,128]{2,1,0:T(8,128)(2,1)S(1)}, bf16[16,128,128]{2,1,0:T(8,128)(2,1)S(1)}, u32[]{:S(2)}, u32[]{:S(2)}) collective-permute-start(bf16[16,128,128]{2,1,0:T(8,128)(2,1)S(1)} %get-tuple-element.167), channel_id=1, source_target_pairs={{0,7},{1,6},{2,5},{3,4},{4,3},{5,2},{6,1},{7,0},{8,15},{9,14},{10,... | collective-permute-start | bytes 1572872 | tf_op jit(solution)/shard_map/ppermute | solution.py:308
  188.0 80.3 %collective-permute-start.35 = (bf16[16,128,128]{2,1,0:T(8,128)(2,1)S(1)}, bf16[16,128,128]{2,1,0:T(8,128)(2,1)S(1)}, u32[]{:S(2)}, u32[]{:S(2)}) collective-permute-start(bf16[16,128,128]{2,1,0:T(8,128)(2,1)S(1)} %get-tuple-element.154), channel_id=1, source_target_pairs={{0,1},{1,0},{2,3},{3,2},{4,5},{5,4},{6,7},{7,6},{8,9},{9,8},{10,11... | collective-permute-start | bytes 1572872 | tf_op jit(solution)/shard_map/ppermute | solution.py:308
  220.4 55.3 %collective-permute-start.36 = (bf16[16,128,128]{2,1,0:T(8,128)(2,1)S(1)}, bf16[16,128,128]{2,1,0:T(8,128)(2,1)S(1)}, u32[]{:S(2)}, u32[]{:S(2)}) collective-permute-start(bf16[16,128,128]{2,1,0:T(8,128)(2,1)S(1)} %get-tuple-element.155), channel_id=1, source_target_pairs={{0,2},{1,3},{2,0},{3,1},{4,6},{5,7},{6,4},{7,5},{8,10},{9,11},{10,... | collective-permute-start | bytes 1572872 | tf_op jit(solution)/shard_map/ppermute | solution.py:308
  231.6 47.0 %collective-permute-start.37 = (bf16[16,128,128]{2,1,0:T(8,128)(2,1)S(1)}, bf16[16,128,128]{2,1,0:T(8,128)(2,1)S(1)}, u32[]{:S(2)}, u32[]{:S(2)}) collective-permute-start(bf16[16,128,128]{2,1,0:T(8,128)(2,1)S(1)} %get-tuple-element.156), channel_id=1, source_target_pairs={{0,3},{1,2},{2,1},{3,0},{4,7},{5,6},{6,5},{7,4},{8,11},{9,10},{10,... | collective-permute-start | bytes 1572872 | tf_op jit(solution)/shard_map/ppermute | solution.py:308
  231.6 80.2 %collective-permute-start.38 = (bf16[16,128,128]{2,1,0:T(8,128)(2,1)S(1)}, bf16[16,128,128]{2,1,0:T(8,128)(2,1)S(1)}, u32[]{:S(2)}, u32[]{:S(2)}) collective-permute-start(bf16[16,128,128]{2,1,0:T(8,128)(2,1)S(1)} %get-tuple-element.157), channel_id=1, source_target_pairs={{0,4},{1,5},{2,6},{3,7},{4,0},{5,1},{6,2},{7,3},{8,12},{9,13},{10,... | collective-permute-start | bytes 1572872 | tf_op jit(solution)/shard_map/ppermute | solution.py:308
  243.7 79.6 %collective-permute-start.39 = (bf16[16,128,128]{2,1,0:T(8,128)(2,1)S(1)}, bf16[16,128,128]{2,1,0:T(8,128)(2,1)S(1)}, u32[]{:S(2)}, u32[]{:S(2)}) collective-permute-start(bf16[16,128,128]{2,1,0:T(8,128)(2,1)S(1)} %get-tuple-element.158), channel_id=1, source_target_pairs={{0,5},{1,4},{2,7},{3,6},{4,1},{5,0},{6,3},{7,2},{8,13},{9,12},{10,... | collective-permute-start | bytes 1572872 | tf_op jit(solution)/shard_map/ppermute | solution.py:308
  269.1 54.9 %collective-permute-start.40 = (bf16[16,128,128]{2,1,0:T(8,128)(2,1)S(1)}, bf16[16,128,128]{2,1,0:T(8,128)(2,1)S(1)}, u32[]{:S(2)}, u32[]{:S(2)}) collective-permute-start(bf16[16,128,128]{2,1,0:T(8,128)(2,1)S(1)} %get-tuple-element.159), channel_id=1, source_target_pairs={{0,6},{1,7},{2,4},{3,5},{4,2},{5,3},{6,0},{7,1},{8,14},{9,15},{10,... | collective-permute-start | bytes 1572872 | tf_op jit(solution)/shard_map/ppermute | solution.py:308
  276.6 59.1 %collective-permute-start.41 = (bf16[16,128,128]{2,1,0:T(8,128)(2,1)S(1)}, bf16[16,128,128]{2,1,0:T(8,128)(2,1)S(1)}, u32[]{:S(2)}, u32[]{:S(2)}) collective-permute-start(bf16[16,128,128]{2,1,0:T(8,128)(2,1)S(1)} %get-tuple-element.160), channel_id=1, source_target_pairs={{0,7},{1,6},{2,5},{3,4},{4,3},{5,2},{6,1},{7,0},{8,15},{9,14},{10,... | collective-permute-start | bytes 1572872 | tf_op jit(solution)/shard_map/ppermute | solution.py:308
  279.4 81.4 %collective-permute-start.28 = (bf16[16,128,128]{2,1,0:T(8,128)(2,1)S(1)}, bf16[16,128,128]{2,1,0:T(8,128)(2,1)S(1)}, u32[]{:S(2)}, u32[]{:S(2)}) collective-permute-start(bf16[16,128,128]{2,1,0:T(8,128)(2,1)S(1)} %get-tuple-element.147), channel_id=1, source_target_pairs={{0,1},{1,0},{2,3},{3,2},{4,5},{5,4},{6,7},{7,6},{8,9},{9,8},{10,11... | collective-permute-start | bytes 1572872 | tf_op jit(solution)/shard_map/ppermute | solution.py:308
  312.5 51.8 %collective-permute-start.29 = (bf16[16,128,128]{2,1,0:T(8,128)(2,1)S(1)}, bf16[16,128,128]{2,1,0:T(8,128)(2,1)S(1)}, u32[]{:S(2)}, u32[]{:S(2)}) collective-permute-start(bf16[16,128,128]{2,1,0:T(8,128)(2,1)S(1)} %get-tuple-element.148), channel_id=1, source_target_pairs={{0,2},{1,3},{2,0},{3,1},{4,6},{5,7},{6,4},{7,5},{8,10},{9,11},{10,... | collective-permute-start | bytes 1572872 | tf_op jit(solution)/shard_map/ppermute | solution.py:308
  324.1 46.8 %collective-permute-start.30 = (bf16[16,128,128]{2,1,0:T(8,128)(2,1)S(1)}, bf16[16,128,128]{2,1,0:T(8,128)(2,1)S(1)}, u32[]{:S(2)}, u32[]{:S(2)}) collective-permute-start(bf16[16,128,128]{2,1,0:T(8,128)(2,1)S(1)} %get-tuple-element.149), channel_id=1, source_target_pairs={{0,3},{1,2},{2,1},{3,0},{4,7},{5,6},{6,5},{7,4},{8,11},{9,10},{10,... | collective-permute-start | bytes 1572872 | tf_op jit(solution)/shard_map/ppermute | solution.py:308
  324.9 79.0 %collective-permute-start.31 = (bf16[16,128,128]{2,1,0:T(8,128)(2,1)S(1)}, bf16[16,128,128]{2,1,0:T(8,128)(2,1)S(1)}, u32[]{:S(2)}, u32[]{:S(2)}) collective-permute-start(bf16[16,128,128]{2,1,0:T(8,128)(2,1)S(1)} %get-tuple-element.150), channel_id=1, source_target_pairs={{0,4},{1,5},{2,6},{3,7},{4,0},{5,1},{6,2},{7,3},{8,12},{9,13},{10,... | collective-permute-start | bytes 1572872 | tf_op jit(solution)/shard_map/ppermute | solution.py:308
  336.4 79.0 %collective-permute-start.32 = (bf16[16,128,128]{2,1,0:T(8,128)(2,1)S(1)}, bf16[16,128,128]{2,1,0:T(8,128)(2,1)S(1)}, u32[]{:S(2)}, u32[]{:S(2)}) collective-permute-start(bf16[16,128,128]{2,1,0:T(8,128)(2,1)S(1)} %get-tuple-element.151), channel_id=1, source_target_pairs={{0,5},{1,4},{2,7},{3,6},{4,1},{5,0},{6,3},{7,2},{8,13},{9,12},{10,... | collective-permute-start | bytes 1572872 | tf_op jit(solution)/shard_map/ppermute | solution.py:308
  361.5 54.7 %collective-permute-start.33 = (bf16[16,128,128]{2,1,0:T(8,128)(2,1)S(1)}, bf16[16,128,128]{2,1,0:T(8,128)(2,1)S(1)}, u32[]{:S(2)}, u32[]{:S(2)}) collective-permute-start(bf16[16,128,128]{2,1,0:T(8,128)(2,1)S(1)} %get-tuple-element.152), channel_id=1, source_target_pairs={{0,6},{1,7},{2,4},{3,5},{4,2},{5,3},{6,0},{7,1},{8,14},{9,15},{10,... | collective-permute-start | bytes 1572872 | tf_op jit(solution)/shard_map/ppermute | solution.py:308
  365.1 62.2 %collective-permute-start.34 = (bf16[16,128,128]{2,1,0:T(8,128)(2,1)S(1)}, bf16[16,128,128]{2,1,0:T(8,128)(2,1)S(1)}, u32[]{:S(2)}, u32[]{:S(2)}) collective-permute-start(bf16[16,128,128]{2,1,0:T(8,128)(2,1)S(1)} %get-tuple-element.153), channel_id=1, source_target_pairs={{0,7},{1,6},{2,5},{3,4},{4,3},{5,2},{6,1},{7,0},{8,15},{9,14},{10,... | collective-permute-start | bytes 1572872 | tf_op jit(solution)/shard_map/ppermute | solution.py:308
  370.9 81.5 %collective-permute-start.21 = (bf16[16,128,128]{2,1,0:T(8,128)(2,1)S(1)}, bf16[16,128,128]{2,1,0:T(8,128)(2,1)S(1)}, u32[]{:S(2)}, u32[]{:S(2)}) collective-permute-start(bf16[16,128,128]{2,1,0:T(8,128)(2,1)S(1)} %get-tuple-element.140), channel_id=1, source_target_pairs={{0,1},{1,0},{2,3},{3,2},{4,5},{5,4},{6,7},{7,6},{8,9},{9,8},{10,11... | collective-permute-start | bytes 1572872 | tf_op jit(solution)/shard_map/ppermute | solution.py:308
  404.6 51.5 %collective-permute-start.22 = (bf16[16,128,128]{2,1,0:T(8,128)(2,1)S(1)}, bf16[16,128,128]{2,1,0:T(8,128)(2,1)S(1)}, u32[]{:S(2)}, u32[]{:S(2)}) collective-permute-start(bf16[16,128,128]{2,1,0:T(8,128)(2,1)S(1)} %get-tuple-element.141), channel_id=1, source_target_pairs={{0,2},{1,3},{2,0},{3,1},{4,6},{5,7},{6,4},{7,5},{8,10},{9,11},{10,... | collective-permute-start | bytes 1572872 | tf_op jit(solution)/shard_map/ppermute | solution.py:308
  416.3 46.3 %collective-permute-start.23 = (bf16[16,128,128]{2,1,0:T(8,128)(2,1)S(1)}, bf16[16,128,128]{2,1,0:T(8,128)(2,1)S(1)}, u32[]{:S(2)}, u32[]{:S(2)}) collective-permute-start(bf16[16,128,128]{2,1,0:T(8,128)(2,1)S(1)} %get-tuple-element.142), channel_id=1, source_target_pairs={{0,3},{1,2},{2,1},{3,0},{4,7},{5,6},{6,5},{7,4},{8,11},{9,10},{10,... | collective-permute-start | bytes 1572872 | tf_op jit(solution)/shard_map/ppermute | solution.py:308
  417.1 78.6 %collective-permute-start.24 = (bf16[16,128,128]{2,1,0:T(8,128)(2,1)S(1)}, bf16[16,128,128]{2,1,0:T(8,128)(2,1)S(1)}, u32[]{:S(2)}, u32[]{:S(2)}) collective-permute-start(bf16[16,128,128]{2,1,0:T(8,128)(2,1)S(1)} %get-tuple-element.143), channel_id=1, source_target_pairs={{0,4},{1,5},{2,6},{3,7},{4,0},{5,1},{6,2},{7,3},{8,12},{9,13},{10,... | collective-permute-start | bytes 1572872 | tf_op jit(solution)/shard_map/ppermute | solution.py:308
  428.1 79.2 %collective-permute-start.25 = (bf16[16,128,128]{2,1,0:T(8,128)(2,1)S(1)}, bf16[16,128,128]{2,1,0:T(8,128)(2,1)S(1)}, u32[]{:S(2)}, u32[]{:S(2)}) collective-permute-start(bf16[16,128,128]{2,1,0:T(8,128)(2,1)S(1)} %get-tuple-element.144), channel_id=1, source_target_pairs={{0,5},{1,4},{2,7},{3,6},{4,1},{5,0},{6,3},{7,2},{8,13},{9,12},{10,... | collective-permute-start | bytes 1572872 | tf_op jit(solution)/shard_map/ppermute | solution.py:308
  453.1 54.2 %collective-permute-start.26 = (bf16[16,128,128]{2,1,0:T(8,128)(2,1)S(1)}, bf16[16,128,128]{2,1,0:T(8,128)(2,1)S(1)}, u32[]{:S(2)}, u32[]{:S(2)}) collective-permute-start(bf16[16,128,128]{2,1,0:T(8,128)(2,1)S(1)} %get-tuple-element.145), channel_id=1, source_target_pairs={{0,6},{1,7},{2,4},{3,5},{4,2},{5,3},{6,0},{7,1},{8,14},{9,15},{10,... | collective-permute-start | bytes 1572872 | tf_op jit(solution)/shard_map/ppermute | solution.py:308
  457.0 69.5 %collective-permute-start.27 = (bf16[16,128,128]{2,1,0:T(8,128)(2,1)S(1)}, bf16[16,128,128]{2,1,0:T(8,128)(2,1)S(1)}, u32[]{:S(2)}, u32[]{:S(2)}) collective-permute-start(bf16[16,128,128]{2,1,0:T(8,128)(2,1)S(1)} %get-tuple-element.146), channel_id=1, source_target_pairs={{0,7},{1,6},{2,5},{3,4},{4,3},{5,2},{6,1},{7,0},{8,15},{9,14},{10,... | collective-permute-start | bytes 1572872 | tf_op jit(solution)/shard_map/ppermute | solution.py:308
  462.6 64.0 %collective-permute-start.14 = (bf16[16,128,128]{2,1,0:T(8,128)(2,1)S(1)}, bf16[16,128,128]{2,1,0:T(8,128)(2,1)S(1)}, u32[]{:S(2)}, u32[]{:S(2)}) collective-permute-start(bf16[16,128,128]{2,1,0:T(8,128)(2,1)S(1)} %get-tuple-element.133), channel_id=1, source_target_pairs={{0,1},{1,0},{2,3},{3,2},{4,5},{5,4},{6,7},{7,6},{8,9},{9,8},{10,11... | collective-permute-start | bytes 1572872 | tf_op jit(solution)/shard_map/ppermute | solution.py:308
  495.7 32.4 %collective-permute-start.15 = (bf16[16,128,128]{2,1,0:T(8,128)(2,1)S(1)}, bf16[16,128,128]{2,1,0:T(8,128)(2,1)S(1)}, u32[]{:S(2)}, u32[]{:S(2)}) collective-permute-start(bf16[16,128,128]{2,1,0:T(8,128)(2,1)S(1)} %get-tuple-element.134), channel_id=1, source_target_pairs={{0,2},{1,3},{2,0},{3,1},{4,6},{5,7},{6,4},{7,5},{8,10},{9,11},{10,... | collective-permute-start | bytes 1572872 | tf_op jit(solution)/shard_map/ppermute | solution.py:308
  507.3 56.7 %collective-permute-start.17 = (bf16[16,128,128]{2,1,0:T(8,128)(2,1)S(1)}, bf16[16,128,128]{2,1,0:T(8,128)(2,1)S(1)}, u32[]{:S(2)}, u32[]{:S(2)}) collective-permute-start(bf16[16,128,128]{2,1,0:T(8,128)(2,1)S(1)} %get-tuple-element.136), channel_id=1, source_target_pairs={{0,4},{1,5},{2,6},{3,7},{4,0},{5,1},{6,2},{7,3},{8,12},{9,13},{10,... | collective-permute-start | bytes 1572872 | tf_op jit(solution)/shard_map/ppermute | solution.py:308
  526.5 38.6 %collective-permute-start.56 = (f32[16,8,128]{2,1,0:T(8,128)S(1)}, f32[16,8,128]{2,1,0:T(8,128)S(1)}, u32[]{:S(2)}, u32[]{:S(2)}) collective-permute-start(f32[16,8,128]{2,1,0:T(8,128)S(1)} %get-tuple-element.177.refs_0_), channel_id=1, source_target_pairs={{0,8},{8,0},{16,24},{24,16},{1,9},{9,1},{17,25},{25,17},{2,10},{10... | collective-permute-start | bytes 196616 | tf_op jit(solution)/shard_map/ppermute | solution.py:298
  526.5 41.6 %collective-permute-start.57 = (f32[16,8,128]{2,1,0:T(8,128)S(1)}, f32[16,8,128]{2,1,0:T(8,128)S(1)}, u32[]{:S(2)}, u32[]{:S(2)}) collective-permute-start(f32[16,8,128]{2,1,0:T(8,128)S(1)} %get-tuple-element.177.refs_0_), channel_id=1, source_target_pairs={{0,16},{8,24},{16,0},{24,8},{1,17},{9,25},{17,1},{25,9},{2,18},{10... | collective-permute-start | bytes 196616 | tf_op jit(solution)/shard_map/ppermute | solution.py:298
  528.1 40.0 %collective-permute-start.58 = (f32[16,8,128]{2,1,0:T(8,128)S(1)}, f32[16,8,128]{2,1,0:T(8,128)S(1)}, u32[]{:S(2)}, u32[]{:S(2)}) collective-permute-start(f32[16,8,128]{2,1,0:T(8,128)S(1)} %get-tuple-element.177.refs_0_), channel_id=1, source_target_pairs={{0,24},{8,16},{16,8},{24,0},{1,25},{9,17},{17,9},{25,1},{2,26},{10... | collective-permute-start | bytes 196616 | tf_op jit(solution)/shard_map/ppermute | solution.py:298
  528.6 91.8 %collective-permute-start.18 = (bf16[16,128,128]{2,1,0:T(8,128)(2,1)S(1)}, bf16[16,128,128]{2,1,0:T(8,128)(2,1)S(1)}, u32[]{:S(2)}, u32[]{:S(2)}) collective-permute-start(bf16[16,128,128]{2,1,0:T(8,128)(2,1)S(1)} %get-tuple-element.137), channel_id=1, source_target_pairs={{0,5},{1,4},{2,7},{3,6},{4,1},{5,0},{6,3},{7,2},{8,13},{9,12},{10,... | collective-permute-start | bytes 1572872 | tf_op jit(solution)/shard_map/ppermute | solution.py:308
  564.0 56.5 %collective-permute-start.19 = (bf16[16,128,128]{2,1,0:T(8,128)(2,1)S(1)}, bf16[16,128,128]{2,1,0:T(8,128)(2,1)S(1)}, u32[]{:S(2)}, u32[]{:S(2)}) collective-permute-start(bf16[16,128,128]{2,1,0:T(8,128)(2,1)S(1)} %get-tuple-element.138), channel_id=1, source_target_pairs={{0,6},{1,7},{2,4},{3,5},{4,2},{5,3},{6,0},{7,1},{8,14},{9,15},{10,... | collective-permute-start | bytes 1572872 | tf_op jit(solution)/shard_map/ppermute | solution.py:308
  565.2 56.8 %collective-permute-start.20 = (bf16[16,128,128]{2,1,0:T(8,128)(2,1)S(1)}, bf16[16,128,128]{2,1,0:T(8,128)(2,1)S(1)}, u32[]{:S(2)}, u32[]{:S(2)}) collective-permute-start(bf16[16,128,128]{2,1,0:T(8,128)(2,1)S(1)} %get-tuple-element.139), channel_id=1, source_target_pairs={{0,7},{1,6},{2,5},{3,4},{4,3},{5,2},{6,1},{7,0},{8,15},{9,14},{10,... | collective-permute-start | bytes 1572872 | tf_op jit(solution)/shard_map/ppermute | solution.py:308
  568.1 85.8 %collective-permute-start.10 = (bf16[16,128,128]{2,1,0:T(8,128)(2,1)S(1)}, bf16[16,128,128]{2,1,0:T(8,128)(2,1)S(1)}, u32[]{:S(2)}, u32[]{:S(2)}) collective-permute-start(bf16[16,128,128]{2,1,0:T(8,128)(2,1)S(1)} %get-tuple-element.129), channel_id=1, source_target_pairs={{0,4},{1,5},{2,6},{3,7},{4,0},{5,1},{6,2},{7,3},{8,12},{9,13},{10,... | collective-permute-start | bytes 1572872 | tf_op jit(solution)/shard_map/ppermute | solution.py:308
  568.1 108.5 %collective-permute-start.11 = (bf16[16,128,128]{2,1,0:T(8,128)(2,1)S(1)}, bf16[16,128,128]{2,1,0:T(8,128)(2,1)S(1)}, u32[]{:S(2)}, u32[]{:S(2)}) collective-permute-start(bf16[16,128,128]{2,1,0:T(8,128)(2,1)S(1)} %get-tuple-element.130), channel_id=1, source_target_pairs={{0,5},{1,4},{2,7},{3,6},{4,1},{5,0},{6,3},{7,2},{8,13},{9,12},{10,... | collective-permute-start | bytes 1572872 | tf_op jit(solution)/shard_map/ppermute | solution.py:308
  620.5 57.9 %collective-permute-start.59 = (f32[16,8,128]{2,1,0:T(8,128)S(1)}, f32[16,8,128]{2,1,0:T(8,128)S(1)}, u32[]{:S(2)}, u32[]{:S(2)}) collective-permute-start(f32[16,8,128]{2,1,0:T(8,128)S(1)} %get-tuple-element.185.refs_0_), channel_id=1, source_target_pairs={{0,8},{8,0},{16,24},{24,16},{1,9},{9,1},{17,25},{25,17},{2,10},{10... | collective-permute-start | bytes 196616 | tf_op jit(solution)/shard_map/ppermute | solution.py:298
  620.5 59.0 %collective-permute-start.60 = (f32[16,8,128]{2,1,0:T(8,128)S(1)}, f32[16,8,128]{2,1,0:T(8,128)S(1)}, u32[]{:S(2)}, u32[]{:S(2)}) collective-permute-start(f32[16,8,128]{2,1,0:T(8,128)S(1)} %get-tuple-element.185.refs_0_), channel_id=1, source_target_pairs={{0,16},{8,24},{16,0},{24,8},{1,17},{9,25},{17,1},{25,9},{2,18},{10... | collective-permute-start | bytes 196616 | tf_op jit(solution)/shard_map/ppermute | solution.py:298
  622.0 57.5 %collective-permute-start.61 = (f32[16,8,128]{2,1,0:T(8,128)S(1)}, f32[16,8,128]{2,1,0:T(8,128)S(1)}, u32[]{:S(2)}, u32[]{:S(2)}) collective-permute-start(f32[16,8,128]{2,1,0:T(8,128)S(1)} %get-tuple-element.185.refs_0_), channel_id=1, source_target_pairs={{0,24},{8,16},{16,8},{24,0},{1,25},{9,17},{17,9},{25,1},{2,26},{10... | collective-permute-start | bytes 196616 | tf_op jit(solution)/shard_map/ppermute | solution.py:298
  653.9 44.6 %collective-permute-start.12 = (bf16[16,128,128]{2,1,0:T(8,128)(2,1)S(1)}, bf16[16,128,128]{2,1,0:T(8,128)(2,1)S(1)}, u32[]{:S(2)}, u32[]{:S(2)}) collective-permute-start(bf16[16,128,128]{2,1,0:T(8,128)(2,1)S(1)} %get-tuple-element.131), channel_id=1, source_target_pairs={{0,6},{1,7},{2,4},{3,5},{4,2},{5,3},{6,0},{7,1},{8,14},{9,15},{10,... | collective-permute-start | bytes 1572872 | tf_op jit(solution)/shard_map/ppermute | solution.py:308
  676.7 21.8 %collective-permute-start.13 = (bf16[16,128,128]{2,1,0:T(8,128)(2,1)S(1)}, bf16[16,128,128]{2,1,0:T(8,128)(2,1)S(1)}, u32[]{:S(2)}, u32[]{:S(2)}) collective-permute-start(bf16[16,128,128]{2,1,0:T(8,128)(2,1)S(1)} %get-tuple-element.132), channel_id=1, source_target_pairs={{0,7},{1,6},{2,5},{3,4},{4,3},{5,2},{6,1},{7,0},{8,15},{9,14},{10,... | collective-permute-start | bytes 1572872 | tf_op jit(solution)/shard_map/ppermute | solution.py:308
  678.4 24.0 %collective-permute-start.7 = (bf16[16,128,128]{2,1,0:T(8,128)(2,1)S(1)}, bf16[16,128,128]{2,1,0:T(8,128)(2,1)S(1)}, u32[]{:S(2)}, u32[]{:S(2)}) collective-permute-start(bf16[16,128,128]{2,1,0:T(8,128)(2,1)S(1)} %get-tuple-element.126), channel_id=1, source_target_pairs={{0,1},{1,0},{2,3},{3,2},{4,5},{5,4},{6,7},{7,6},{8,9},{9,8},{10,11... | collective-permute-start | bytes 1572872 | tf_op jit(solution)/shard_map/ppermute | solution.py:308
  679.5 24.0 %collective-permute-start.8 = (bf16[16,128,128]{2,1,0:T(8,128)(2,1)S(1)}, bf16[16,128,128]{2,1,0:T(8,128)(2,1)S(1)}, u32[]{:S(2)}, u32[]{:S(2)}) collective-permute-start(bf16[16,128,128]{2,1,0:T(8,128)(2,1)S(1)} %get-tuple-element.127), channel_id=1, source_target_pairs={{0,2},{1,3},{2,0},{3,1},{4,6},{5,7},{6,4},{7,5},{8,10},{9,11},{10,... | collective-permute-start | bytes 1572872 | tf_op jit(solution)/shard_map/ppermute | solution.py:308
  679.5 40.0 %collective-permute-start.9 = (bf16[16,128,128]{2,1,0:T(8,128)(2,1)S(1)}, bf16[16,128,128]{2,1,0:T(8,128)(2,1)S(1)}, u32[]{:S(2)}, u32[]{:S(2)}) collective-permute-start(bf16[16,128,128]{2,1,0:T(8,128)(2,1)S(1)} %get-tuple-element.128), channel_id=1, source_target_pairs={{0,3},{1,2},{2,1},{3,0},{4,7},{5,6},{6,5},{7,4},{8,11},{9,10},{10,... | collective-permute-start | bytes 1572872 | tf_op jit(solution)/shard_map/ppermute | solution.py:308
  698.5 24.0 %collective-permute-start.62 = (f32[16,8,128]{2,1,0:T(8,128)S(1)}, f32[16,8,128]{2,1,0:T(8,128)S(1)}, u32[]{:S(2)}, u32[]{:S(2)}) collective-permute-start(f32[16,8,128]{2,1,0:T(8,128)S(1)} %get-tuple-element.193.refs_0_), channel_id=1, source_target_pairs={{0,8},{8,0},{16,24},{24,16},{1,9},{9,1},{17,25},{25,17},{2,10},{10... | collective-permute-start | bytes 196616 | tf_op jit(solution)/shard_map/ppermute | solution.py:298
  698.5 24.2 %collective-permute-start.63 = (f32[16,8,128]{2,1,0:T(8,128)S(1)}, f32[16,8,128]{2,1,0:T(8,128)S(1)}, u32[]{:S(2)}, u32[]{:S(2)}) collective-permute-start(f32[16,8,128]{2,1,0:T(8,128)S(1)} %get-tuple-element.193.refs_0_), channel_id=1, source_target_pairs={{0,16},{8,24},{16,0},{24,8},{1,17},{9,25},{17,1},{25,9},{2,18},{10... | collective-permute-start | bytes 196616 | tf_op jit(solution)/shard_map/ppermute | solution.py:298
  702.4 25.3 %collective-permute-start.64 = (f32[16,8,128]{2,1,0:T(8,128)S(1)}, f32[16,8,128]{2,1,0:T(8,128)S(1)}, u32[]{:S(2)}, u32[]{:S(2)}) collective-permute-start(f32[16,8,128]{2,1,0:T(8,128)S(1)} %get-tuple-element.193.refs_0_), channel_id=1, source_target_pairs={{0,24},{8,16},{16,8},{24,0},{1,25},{9,17},{17,9},{25,1},{2,26},{10... | collective-permute-start | bytes 196616 | tf_op jit(solution)/shard_map/ppermute | solution.py:298
  703.4 40.9 %collective-permute-start.77 = (bf16[8,128,128]{2,1,0:T(8,128)(2,1)S(1)}, bf16[8,128,128]{2,1,0:T(8,128)(2,1)S(1)}, u32[]{:S(2)}, u32[]{:S(2)}) collective-permute-start(bf16[8,128,128]{2,1,0:T(8,128)(2,1)S(1)} %get-tuple-element.212), channel_id=1, source_target_pairs={{0,3},{1,2},{2,1},{3,0},{4,7},{5,6},{6,5},{7,4},{8,11},{9,10},{10,... | collective-permute-start | bytes 786440 | tf_op jit(solution)/shard_map/ppermute | solution.py:308
  719.5 24.8 %collective-permute-start.78 = (bf16[8,128,128]{2,1,0:T(8,128)(2,1)S(1)}, bf16[8,128,128]{2,1,0:T(8,128)(2,1)S(1)}, u32[]{:S(2)}, u32[]{:S(2)}) collective-permute-start(bf16[8,128,128]{2,1,0:T(8,128)(2,1)S(1)} %get-tuple-element.213), channel_id=1, source_target_pairs={{0,4},{1,5},{2,6},{3,7},{4,0},{5,1},{6,2},{7,3},{8,12},{9,13},{10,... | collective-permute-start | bytes 786440 | tf_op jit(solution)/shard_map/ppermute | solution.py:308
  722.5 35.4 %collective-permute-start.79 = (bf16[8,128,128]{2,1,0:T(8,128)(2,1)S(1)}, bf16[8,128,128]{2,1,0:T(8,128)(2,1)S(1)}, u32[]{:S(2)}, u32[]{:S(2)}) collective-permute-start(bf16[8,128,128]{2,1,0:T(8,128)(2,1)S(1)} %get-tuple-element.214), channel_id=1, source_target_pairs={{0,5},{1,4},{2,7},{3,6},{4,1},{5,0},{6,3},{7,2},{8,13},{9,12},{10,... | collective-permute-start | bytes 786440 | tf_op jit(solution)/shard_map/ppermute | solution.py:308
  722.7 35.2 %collective-permute-start.80 = (bf16[8,128,128]{2,1,0:T(8,128)(2,1)S(1)}, bf16[8,128,128]{2,1,0:T(8,128)(2,1)S(1)}, u32[]{:S(2)}, u32[]{:S(2)}) collective-permute-start(bf16[8,128,128]{2,1,0:T(8,128)(2,1)S(1)} %get-tuple-element.215), channel_id=1, source_target_pairs={{0,6},{1,7},{2,4},{3,5},{4,2},{5,3},{6,0},{7,1},{8,14},{9,15},{10,... | collective-permute-start | bytes 786440 | tf_op jit(solution)/shard_map/ppermute | solution.py:308
  727.7 31.5 %collective-permute-start.81 = (bf16[8,128,128]{2,1,0:T(8,128)(2,1)S(1)}, bf16[8,128,128]{2,1,0:T(8,128)(2,1)S(1)}, u32[]{:S(2)}, u32[]{:S(2)}) collective-permute-start(bf16[8,128,128]{2,1,0:T(8,128)(2,1)S(1)} %get-tuple-element.216), channel_id=1, source_target_pairs={{0,7},{1,6},{2,5},{3,4},{4,3},{5,2},{6,1},{7,0},{8,15},{9,14},{10,... | collective-permute-start | bytes 786440 | tf_op jit(solution)/shard_map/ppermute | solution.py:308
  (125 other events, 2578.7 us)
